TPU v7x, 32 devices: a whole 2x2x4 slice. The times are simulated.
32 devices in a mesh: group: 2 (over y), hi: 4 (over z), lo: 2 (over x), cuts: 2 (over core).
Axes of the slice: x: 2, y: 2, z: 4, core: 2. Of those that a mesh axis runs over, the one named last changes fastest.
Arguments:
- state_block: float32 [8, 2, 131072], P(('group', 'hi'), 'lo'), parts along dimension 0, may hold values from -6 to 6
- gate_table: float32 [4, 256, 256], replicated, may hold values from -0.375 to 0.375
- closing_table: float32 [4, 2, 2, 256], replicated, may hold values from -1 to 1
- slice_edges: int32 [8, 3], P(('group', 'cuts')), parts along dimension 0, may hold values from 0 to 3
- bit_orders: int32 [2, 8], replicated, may hold values from 0 to 7, each once within a row
Outputs:
- amplitudes: float32 [8, 2, 65536], P(('group', 'hi'), 'lo', 'cuts'), parts along dimension 0
There are 2 independent parts, one for each index of `group`. A program takes and returns all parts, laid end to end along the dimension named above; an argument that names none is the same for every part. Nothing has to cross between parts.
Inputs may be any that keep to these rules, and one draw needn't show every extreme that they name: `bit_orders`: each row is a permutation of 0 to 7.
All inputs are finite; a program needn't handle non-finite values.
Results may differ from a plain program's by a relative error of at most 0.0001.
Values sent between devices are 32-bit elements; how exact they have to be, the bound alone decides.
A program may use at most 64 MiB of HBM per device.

v0:
```python
import functools

import jax
import jax.numpy as jnp
from jax import lax
from jax.experimental import pallas as pl
from jax.experimental.pallas import tpu as pltpu
from jax.sharding import PartitionSpec as P

BITS = 8
GATE = 256
CLOSED = 2


def permuted(gate, order):
    rows = jnp.arange(GATE, dtype=jnp.int32)
    picked = rows[:, None] >> order[None, :] & 1
    weights = jnp.left_shift(jnp.ones((BITS,), jnp.int32), jnp.arange(BITS, dtype=jnp.int32))
    source = jnp.sum(picked * weights[None, :], axis=1)
    return jnp.take(gate, source, axis=0)


def local_plain(state_block, gate_table, closing_table, slice_edges, bit_orders):
    count_hi = lax.axis_size("hi")
    count_lo = lax.axis_size("lo")
    span_hi = GATE // count_hi
    span_lo = GATE // count_lo
    middle = state_block.shape[2] // (GATE * GATE * CLOSED)
    tensor = state_block.reshape(span_hi, count_hi, CLOSED, middle, count_lo, span_lo)
    turns = slice_edges.shape[0]
    firsts = []
    seconds = []
    fronts = []
    rears = []
    for turn_index in range(turns):
        chosen = slice_edges[turn_index]
        firsts.append(permuted(gate_table[chosen[0]], bit_orders[0]))
        seconds.append(permuted(gate_table[chosen[1]], bit_orders[1]))
        fronts.append(closing_table[chosen[2], 0])
        rears.append(closing_table[chosen[2], 1])
    section_ones = []
    for turn_index in range(turns):

        def apply_first(piece, first=firsts[turn_index], front=fronts[turn_index]):
            shape = piece.shape
            flat = piece.reshape(GATE, -1)
            product = lax.dot_general(
                first,
                flat,
                (((0,), (0,)), ((), ())),
                precision=lax.Precision.HIGHEST,
                preferred_element_type=jnp.float32,
            )
            scaled = jnp.transpose(front).reshape(shape[0], shape[1], shape[2], 1, 1, 1)
            return product.reshape(shape) * scaled

        section_ones.append(
            apply_first(lax.all_to_all(tensor, "hi", split_axis=1, concat_axis=1, tiled=True))
        )
    total = jnp.zeros((span_hi, count_hi, middle, count_lo, span_lo), jnp.float32)
    for turn_index in range(turns):
        current = section_ones[turn_index]

        def apply_second(piece, second=seconds[turn_index], rear=rears[turn_index]):
            shape = piece.shape
            flat = piece.reshape(-1, GATE)
            product = jnp.dot(
                flat, second, precision=lax.Precision.HIGHEST, preferred_element_type=jnp.float32
            )
            product = product.reshape(shape[0], shape[1], shape[2], shape[3], GATE)
            closed = jnp.einsum("phzkg,zg->phkg", product, rear, precision=lax.Precision.HIGHEST)
            return closed.reshape(shape[0], shape[1], shape[3], shape[4], shape[5])

        total = total + apply_second(
            lax.all_to_all(current, "lo", split_axis=4, concat_axis=4, tiled=True)
        )
    placed = lax.all_to_all(
        lax.all_to_all(total, "hi", split_axis=1, concat_axis=1, tiled=True),
        "lo",
        split_axis=3,
        concat_axis=3,
        tiled=True,
    )
    summed = lax.psum_scatter(placed.reshape(-1), "cuts", scatter_dimension=0, tiled=True)
    return summed.reshape(1, 1, -1)


MESH = pl.DeviceIdType.MESH
HALF = jnp.bfloat16
FULL = jnp.float32


def dot(left, right, dims=((1,), (0,))):
    return lax.dot_general(left, right, (dims, ((), ())), preferred_element_type=FULL)


def halves(value):
    high = value.astype(HALF)
    return high, (value - high.astype(FULL)).astype(HALF)


def source_row(index, orders_ref, section):
    total = jnp.zeros_like(index)
    for bit in range(BITS):
        picked = lax.shift_right_logical(index, jnp.full_like(index, orders_ref[section, bit])) & 1
        total = total | (picked << bit)
    return total


def flipped(index, mask):
    bit = 1
    while bit <= mask:
        if mask & bit:
            index = index + bit - 2 * bit * (index // bit % 2)
        bit *= 2
    return index


def kernel(
    group,
    order,
    count_hi,
    count_lo,
    x_hbm,
    gate_hbm,
    closing_hbm,
    edges_hbm,
    orders_hbm,
    out_ref,
    x_ref,
    gate_ref,
    closing_ref,
    edges_ref,
    orders_ref,
    outgoing,
    arrived,
    edges_far,
    first_ref,
    second_ref,
    sums,
    part_near,
    part_far,
    result,
    landed,
    local_sems,
    edge_sems,
    part_sems,
    in_send,
    in_recv,
    out_send,
    out_recv,
):
    hi, lo, cut = lax.axis_index("hi"), lax.axis_index("lo"), lax.axis_index("cuts")
    other = 1 - cut
    span_hi, span_lo = GATE // count_hi, GATE // count_lo
    rows = GATE // 2
    turns = edges_ref.shape[0]
    edges = gate_ref.shape[0]
    offsets = [
        (a, b) for a in range(count_hi) for b in range(count_lo) if a or b
    ]
    pairs = (
        (x_hbm, x_ref),
        (edges_hbm, edges_ref),
        (orders_hbm, orders_ref),
        (closing_hbm, closing_ref),
        (gate_hbm, gate_ref),
    )
    gets = [pltpu.make_async_copy(*pair, local_sems.at[i]) for i, pair in enumerate(pairs)]
    for get in gets:
        get.start()

    def target(a, b):
        return flipped(hi, a), flipped(lo, b)

    barrier = pltpu.get_barrier_semaphore()
    for a, b in offsets:
        th, tl = target(a, b)
        pl.semaphore_signal(barrier, inc=1, device_id={"hi": th, "lo": tl}, device_id_type=MESH)
    pl.semaphore_signal(barrier, inc=1, device_id={"cuts": other}, device_id_type=MESH)

    gets[0].wait()
    stride = count_hi * CLOSED * count_lo
    for b in range(count_hi):
        for e in range(count_lo):
            start = b * CLOSED * count_lo + cut * count_lo + e
            outgoing[b * count_lo + e] = x_ref[pl.ds(start, span_hi, stride=stride), :]
    arrived[lo, pl.ds(pl.multiple_of(hi * span_hi, span_hi), span_hi), :] = outgoing[
        hi * count_lo + lo
    ]
    pl.semaphore_wait(barrier, len(offsets) + 1)

    sends = []
    for k, (a, b) in enumerate(offsets):
        th, tl = target(a, b)
        copy = pltpu.make_async_remote_copy(
            src_ref=outgoing.at[th * count_lo + tl],
            dst_ref=arrived.at[lo, pl.ds(pl.multiple_of(hi * span_hi, span_hi), span_hi), :],
            send_sem=in_send.at[k],
            recv_sem=in_recv.at[k],
            device_id={"hi": th, "lo": tl},
            device_id_type=MESH,
        )
        sends.append(copy)
    for k in [0] + list(range(len(offsets) - 1, 0, -1)):
        sends[k].start()
    gets[1].wait()
    edge_copy = pltpu.make_async_remote_copy(
        src_ref=edges_ref,
        dst_ref=edges_far,
        send_sem=edge_sems.at[0],
        recv_sem=edge_sems.at[1],
        device_id={"cuts": other},
        device_id_type=MESH,
    )
    edge_copy.start()

    gets[2].wait()
    down = lax.broadcasted_iota(jnp.int32, (GATE, GATE), 0)
    along = lax.broadcasted_iota(jnp.int32, (GATE, GATE), 1)
    per = span_hi // 2
    wide = group * span_hi
    column = (down // rows * per + down % per) * count_hi + down % rows // per
    columns = (column == along).astype(FULL).astype(HALF)
    rows_one = source_row(along % span_hi * count_hi + along // span_hi, orders_ref, 0)
    rows_one = (rows_one == down).astype(FULL).astype(HALF)
    rows_two = (source_row(down, orders_ref, 1) == along).astype(FULL).astype(HALF)

    gets[3].wait()
    gets[4].wait()
    edge_copy.wait()
    for s in range(2 * turns):
        chosen = edges_ref if s < turns else edges_far
        turn = s % turns

        def pick(place, values):
            total = None
            for c in range(edges):
                weight = (chosen[turn : turn + 1, place : place + 1] == c).astype(FULL)
                term = weight * values(c)
                total = term if total is None else total + term
            return total

        front = pick(2, lambda c: closing_ref[c, 0, pl.ds(cut, 1), :])
        rear = pick(2, lambda c: closing_ref[c, 1, pl.ds(cut, 1), :])
        for part, piece in enumerate(halves(pick(0, lambda c: gate_ref[c]) * front)):
            moved = dot(columns, piece, ((1,), (1,))).astype(HALF)
            moved = dot(moved, rows_one).astype(HALF)
            for side in range(2):
                for c in range(count_hi // group):
                    first_ref[part, c, side, :, s * wide : (s + 1) * wide] = moved[
                        side * rows : (side + 1) * rows, c * wide : (c + 1) * wide
                    ]
        for part, piece in enumerate(halves(pick(1, lambda c: gate_ref[c]) * rear)):
            second_ref[part, s] = dot(rows_two, piece).astype(HALF)

    def advance(step):
        for copy, (a, b) in zip(sends, offsets):
            if a // group == step:
                copy.wait_recv()
        c = flipped(hi // group, step)
        place = pl.ds(pl.multiple_of(c * wide, wide), wide)
        piece = jnp.concatenate([arrived[i, place, :] for i in range(count_lo)], axis=1)
        high, low = halves(piece)
        inner = []
        for s in range(2 * turns):
            inner.append(
                dot(high, second_ref[0, s]) + dot(low, second_ref[0, s]) + dot(high, second_ref[1, s])
            )
        high, low = halves(jnp.concatenate(inner, axis=0))

        def side_sum(side):
            left, rest = first_ref[0, c, side], first_ref[1, c, side]
            return dot(left, high) + dot(left, low) + dot(rest, high)

        return side_sum

    for i, step in enumerate(order[:-1]):
        side_sum = advance(step)
        for side in range(2):
            if i == 0:
                sums[side] = side_sum(side)
            else:
                sums[side] += side_sum(side)
    side_sum = advance(order[-1])
    part_near[...] = sums[other] + side_sum(other)
    part_copy = pltpu.make_async_remote_copy(
        src_ref=part_near,
        dst_ref=part_far,
        send_sem=part_sems.at[0],
        recv_sem=part_sems.at[1],
        device_id={"cuts": other},
        device_id_type=MESH,
    )
    part_copy.start()
    own = sums[cut] + side_sum(cut)
    part_copy.wait_recv()
    own = own + part_far[...]
    for b in range(count_hi):
        for e in range(count_lo):
            result[b * count_lo + e] = own[b * per : (b + 1) * per, e * span_lo : (e + 1) * span_lo]
    here = hi * count_lo + lo
    outs = []
    for k, (a, b) in enumerate(offsets):
        th, tl = target(a, b)
        copy = pltpu.make_async_remote_copy(
            src_ref=result.at[th * count_lo + tl],
            dst_ref=landed.at[here],
            send_sem=out_send.at[k],
            recv_sem=out_recv.at[k],
            device_id={"hi": th, "lo": tl},
            device_id_type=MESH,
        )
        outs.append(copy)
    for k in range(len(offsets) - 1, -1, -1):
        outs[k].start()
    blocks = count_hi * count_lo
    out_ref[pl.ds(here, per, stride=blocks), :] = result[here]
    for copy, (a, b) in zip(outs, offsets):
        copy.wait_recv()
        th, tl = target(a, b)
        j = th * count_lo + tl
        out_ref[pl.ds(j, per, stride=blocks), :] = landed[j]
    for copy in sends:
        copy.wait_send()
    part_copy.wait_send()
    for copy in outs:
        copy.wait_send()


def local(state_block, gate_table, closing_table, slice_edges, bit_orders):
    count_hi = lax.axis_size("hi")
    count_lo = lax.axis_size("lo")
    span_hi = GATE // count_hi
    span_lo = GATE // count_lo
    blocks = count_hi * count_lo
    middle = state_block.shape[2] // (GATE * GATE * CLOSED)
    fits = middle == 1 and span_lo == 128 and span_hi % 16 == 0
    if not fits or lax.axis_size("cuts") != CLOSED:
        return local_plain(state_block, gate_table, closing_table, slice_edges, bit_orders)
    group = 1
    order = (0, 1, 3, 2) if count_hi == 4 else tuple(range(count_hi // group))
    slices = slice_edges.shape[0] * CLOSED
    rows = GATE // 2
    hbm = pl.BlockSpec(memory_space=pltpu.HBM)
    dma = pltpu.SemaphoreType.DMA
    out = pl.pallas_call(
        functools.partial(kernel, group, order, count_hi, count_lo),
        out_shape=jax.ShapeDtypeStruct((span_hi // 2 * blocks, span_lo), FULL),
        in_specs=[hbm] * 5,
        out_specs=pl.BlockSpec(memory_space=pltpu.VMEM),
        scratch_shapes=[
            pltpu.VMEM((span_hi * blocks * CLOSED, span_lo), FULL),
            pltpu.VMEM(gate_table.shape, FULL),
            pltpu.VMEM(closing_table.shape, FULL),
            pltpu.VMEM(slice_edges.shape, jnp.int32),
            pltpu.SMEM(bit_orders.shape, jnp.int32),
            pltpu.VMEM((blocks, span_hi, span_lo), FULL),
            pltpu.VMEM((count_lo, GATE, span_lo), FULL),
            pltpu.VMEM(slice_edges.shape, jnp.int32),
            pltpu.VMEM((2, count_hi // group, 2, rows, slices * group * span_hi), HALF),
            pltpu.VMEM((2, slices, GATE, GATE), HALF),
            pltpu.VMEM((2, rows, GATE), FULL),
            pltpu.VMEM((rows, GATE), FULL),
            pltpu.VMEM((rows, GATE), FULL),
            pltpu.VMEM((blocks, span_hi // 2, span_lo), FULL),
            pltpu.VMEM((blocks, span_hi // 2, span_lo), FULL),
            dma((5,)),
            dma((2,)),
            dma((2,)),
            dma((blocks,)),
            dma((blocks,)),
            dma((blocks,)),
            dma((blocks,)),
        ],
        compiler_params=pltpu.CompilerParams(
            collective_id=0, has_side_effects=True, vmem_limit_bytes=32 * 1024 * 1024
        ),
    )(
        *(
            pltpu.with_memory_space_constraint(item, pltpu.HBM)
            for item in (
                state_block.reshape(-1, span_lo),
                gate_table,
                closing_table,
                slice_edges,
                bit_orders,
            )
        )
    )
    return out.reshape(1, 1, -1)


def solution(mesh):
    in_specs = (P(("group", "hi"), "lo", None), P(), P(), P(("group", "cuts"), None), P())
    out_specs = P(("group", "hi"), "lo", "cuts")
    return jax.shard_map(local, mesh=mesh, in_specs=in_specs, out_specs=out_specs, check_vma=False)
```

profile of v0, /device:TPU:1, one launch (start us, length us, event | category | flops | bytes accessed | tf_op | source)
XLA Modules:
  0.0 19.7 jit_solution(10710615069611445440)
XLA Ops:
  0.0 19.0 %shard_map.55 = f32[256,128]{1,0:T(8,128)S(1)} custom-call(f32[1024,128]{1,0:T(8,128)} %bitcast.3, f32[4,256,256]{2,1,0:T(8,128)} %gate_hbm.1, f32[4,2,2,256]{3,2,1,0:T(2,128)} %closing_hbm.1, s32[2,3]{1,0:T(2,128)} %edges_hbm.1, s32[2,8]{1,0:T(2,128)} %orders_hbm.1), custom_call_target="tpu_custom_call" | custom-call | tf_op jit(solution)/shard_map/pallas_call | solution.py:347
  19.0 0.7 %copy.7 = f32[1,1,32768]{2,1,0:T(1,128)} copy(f32[1,1,32768]{2,1,0:T(1,128)S(1)} %bitcast.2) | data formatting | bytes 262144
where the time goes:
time: 19.8 us; the launch traced here: 19.7 us
  Pallas kernels  19 us (96%)
  local copies, waits for them, and re-layouts  0.66 us (3%)
    pallas_call x1, Pallas kernels, local(): pl.pallas_call(functools.partial(kernel, group, order, count_hi, count_lo...  19 us
    unnamed x1, local copies, waits for them, and re-layouts  0.66 us

commit v1 on v0

v1 whole, which is shorter than its diff:
```python
import functools

import jax
import jax.numpy as jnp
from jax import lax
from jax.experimental import pallas as pl
from jax.experimental.pallas import tpu as pltpu
from jax.sharding import PartitionSpec as P

BITS = 8
GATE = 256
CLOSED = 2


def permuted(gate, order):
    rows = jnp.arange(GATE, dtype=jnp.int32)
    picked = rows[:, None] >> order[None, :] & 1
    weights = jnp.left_shift(jnp.ones((BITS,), jnp.int32), jnp.arange(BITS, dtype=jnp.int32))
    source = jnp.sum(picked * weights[None, :], axis=1)
    return jnp.take(gate, source, axis=0)


def local_plain(state_block, gate_table, closing_table, slice_edges, bit_orders):
    count_hi = lax.axis_size("hi")
    count_lo = lax.axis_size("lo")
    span_hi = GATE // count_hi
    span_lo = GATE // count_lo
    middle = state_block.shape[2] // (GATE * GATE * CLOSED)
    tensor = state_block.reshape(span_hi, count_hi, CLOSED, middle, count_lo, span_lo)
    turns = slice_edges.shape[0]
    firsts = []
    seconds = []
    fronts = []
    rears = []
    for turn_index in range(turns):
        chosen = slice_edges[turn_index]
        firsts.append(permuted(gate_table[chosen[0]], bit_orders[0]))
        seconds.append(permuted(gate_table[chosen[1]], bit_orders[1]))
        fronts.append(closing_table[chosen[2], 0])
        rears.append(closing_table[chosen[2], 1])
    section_ones = []
    for turn_index in range(turns):

        def apply_first(piece, first=firsts[turn_index], front=fronts[turn_index]):
            shape = piece.shape
            flat = piece.reshape(GATE, -1)
            product = lax.dot_general(
                first,
                flat,
                (((0,), (0,)), ((), ())),
                precision=lax.Precision.HIGHEST,
                preferred_element_type=jnp.float32,
            )
            scaled = jnp.transpose(front).reshape(shape[0], shape[1], shape[2], 1, 1, 1)
            return product.reshape(shape) * scaled

        section_ones.append(
            apply_first(lax.all_to_all(tensor, "hi", split_axis=1, concat_axis=1, tiled=True))
        )
    total = jnp.zeros((span_hi, count_hi, middle, count_lo, span_lo), jnp.float32)
    for turn_index in range(turns):
        current = section_ones[turn_index]

        def apply_second(piece, second=seconds[turn_index], rear=rears[turn_index]):
            shape = piece.shape
            flat = piece.reshape(-1, GATE)
            product = jnp.dot(
                flat, second, precision=lax.Precision.HIGHEST, preferred_element_type=jnp.float32
            )
            product = product.reshape(shape[0], shape[1], shape[2], shape[3], GATE)
            closed = jnp.einsum("phzkg,zg->phkg", product, rear, precision=lax.Precision.HIGHEST)
            return closed.reshape(shape[0], shape[1], shape[3], shape[4], shape[5])

        total = total + apply_second(
            lax.all_to_all(current, "lo", split_axis=4, concat_axis=4, tiled=True)
        )
    placed = lax.all_to_all(
        lax.all_to_all(total, "hi", split_axis=1, concat_axis=1, tiled=True),
        "lo",
        split_axis=3,
        concat_axis=3,
        tiled=True,
    )
    summed = lax.psum_scatter(placed.reshape(-1), "cuts", scatter_dimension=0, tiled=True)
    return summed.reshape(1, 1, -1)


MESH = pl.DeviceIdType.MESH
HALF = jnp.bfloat16
FULL = jnp.float32


def dot(left, right, dims=((1,), (0,))):
    return lax.dot_general(left, right, (dims, ((), ())), preferred_element_type=FULL)


def halves(value):
    high = value.astype(HALF)
    return high, (value - high.astype(FULL)).astype(HALF)


def source_row(index, orders_ref, section):
    total = jnp.zeros_like(index)
    for bit in range(BITS):
        picked = lax.shift_right_logical(index, jnp.full_like(index, orders_ref[section, bit])) & 1
        total = total | (picked << bit)
    return total


def flipped(index, mask):
    bit = 1
    while bit <= mask:
        if mask & bit:
            index = index + bit - 2 * bit * (index // bit % 2)
        bit *= 2
    return index


def kernel(
    count_hi,
    count_lo,
    x_hbm,
    gate_hbm,
    closing_hbm,
    edges_hbm,
    orders_hbm,
    out_ref,
    x_ref,
    gate_ref,
    closing_ref,
    edges_ref,
    orders_ref,
    outgoing,
    arrived,
    edges_far,
    first_ref,
    second_ref,
    sums,
    result,
    landed,
    local_sems,
    edge_sems,
    ready,
    in_send,
    in_recv,
    out_send,
    out_recv,
):
    hi, lo, cut = lax.axis_index("hi"), lax.axis_index("lo"), lax.axis_index("cuts")
    other = 1 - cut
    span_hi, span_lo = GATE // count_hi, GATE // count_lo
    half = count_hi // 2
    upper, inner = hi // half, hi % half
    rows = GATE // 2
    per = span_hi // 2
    blocks = count_hi * count_lo
    turns = edges_ref.shape[0]
    edges = gate_ref.shape[0]
    near = [(a, b) for a in range(half) for b in range(count_lo)]
    pairs = (
        (x_hbm, x_ref),
        (edges_hbm, edges_ref),
        (orders_hbm, orders_ref),
        (closing_hbm, closing_ref),
        (gate_hbm, gate_ref),
    )
    gets = [pltpu.make_async_copy(*pair, local_sems.at[i]) for i, pair in enumerate(pairs)]
    for get in gets:
        get.start()

    def device(side, a, b, core):
        th = flipped(upper, side) * half + flipped(inner, a)
        return {"hi": th, "lo": flipped(lo, b), "cuts": core}

    def block(a, b, core):
        return (flipped(inner, a) * CLOSED + core) * count_lo + flipped(lo, b)

    def greet(semaphore, side):
        for a, b in near:
            for core in range(CLOSED):
                if side or a or b:
                    pl.semaphore_signal(
                        semaphore, inc=1, device_id=device(side, a, b, core), device_id_type=MESH
                    )

    barrier = pltpu.get_barrier_semaphore()
    pl.semaphore_signal(barrier, inc=1, device_id={"cuts": other}, device_id_type=MESH)
    greet(barrier, 0)

    @pl.when(upper == 0)
    def _():
        greet(barrier, 1)

    gets[0].wait()
    stride = count_hi * CLOSED * count_lo
    for b in range(count_hi):
        for e in range(count_lo):
            start = b * CLOSED * count_lo + cut * count_lo + e
            outgoing[b * count_lo + e] = x_ref[pl.ds(start, span_hi, stride=stride), :]
    arrived[0, 0, cut] = outgoing[block(0, 0, cut)]
    pl.semaphore_wait(barrier, blocks - 1 + upper * blocks)

    sends = []
    for core in range(CLOSED):
        for a, b in sorted(near[1:], key=lambda spot: (spot[0] > 0, spot[1] == 0)):
            k = a * count_lo + b
            copy = pltpu.make_async_remote_copy(
                src_ref=outgoing.at[block(a, b, core)],
                dst_ref=arrived.at[a, b, cut],
                send_sem=in_send.at[core, k],
                recv_sem=in_recv.at[cut, k],
                device_id=device(0, a, b, core),
                device_id_type=MESH,
            )
            copy.start()
            sends.append(copy)
    copy = pltpu.make_async_remote_copy(
        src_ref=outgoing.at[block(0, 0, other)],
        dst_ref=arrived.at[0, 0, cut],
        send_sem=in_send.at[0, 0],
        recv_sem=in_recv.at[cut, 0],
        device_id={"cuts": other},
        device_id_type=MESH,
    )
    copy.start()
    sends.append(copy)

    gets[1].wait()
    edge_copy = pltpu.make_async_remote_copy(
        src_ref=edges_ref,
        dst_ref=edges_far,
        send_sem=edge_sems.at[0],
        recv_sem=edge_sems.at[1],
        device_id={"cuts": other},
        device_id_type=MESH,
    )
    edge_copy.start()

    @pl.when(upper == 1)
    def _():
        greet(ready, 1)

    gets[2].wait()
    down = lax.broadcasted_iota(jnp.int32, (GATE, GATE), 0)
    along = lax.broadcasted_iota(jnp.int32, (GATE, GATE), 1)

    def high_bits(side, a):
        return (side ^ upper) * half + (a ^ inner)

    column = down % span_hi * count_hi + high_bits(down // rows, down % rows // span_hi)
    columns = (column == along).astype(FULL).astype(HALF)
    row = down % span_hi * count_hi + high_bits(0, down % rows // span_hi)
    rows_one = (source_row(row[:rows], orders_ref, 0) == along[:rows]).astype(FULL).astype(HALF)
    row = (down // span_lo ^ lo) * span_lo + down % span_lo
    rows_two = (source_row(row, orders_ref, 1) == along).astype(FULL).astype(HALF)

    gets[3].wait()
    gets[4].wait()
    edge_copy.wait()
    wide = CLOSED * span_hi
    rears = []
    for s in range(2 * turns):
        chosen = edges_ref if s < turns else edges_far
        turn = s % turns

        def pick(place, values):
            total = None
            for c in range(edges):
                weight = (chosen[turn : turn + 1, place : place + 1] == c).astype(FULL)
                term = weight * values(c)
                total = term if total is None else total + term
            return total

        rears.append(pick(2, lambda c: closing_ref[c, 1]))
        fronts = pick(2, lambda c: closing_ref[c, 0])
        gate = pick(0, lambda c: gate_ref[c])
        split = [halves(gate * fronts[z : z + 1]) for z in range(CLOSED)]
        for part in range(2):
            moved = [dot(rows_one, split[z][part]).astype(HALF) for z in range(CLOSED)]
            moved = dot(columns, jnp.concatenate(moved, axis=0), ((1,), (1,))).astype(HALF)
            for side in range(2):
                for a in range(half):
                    for z in range(CLOSED):
                        start = z * rows + a * span_hi
                        first_ref[
                            part, a, side, :, s * wide + z * span_hi : s * wide + (z + 1) * span_hi
                        ] = moved[side * rows : (side + 1) * rows, start : start + span_hi]
        for part, piece in enumerate(halves(pick(1, lambda c: gate_ref[c]))):
            second_ref[part, s] = dot(rows_two, piece).astype(HALF)

    def advance(a):
        for b in range(count_lo):
            for core in range(CLOSED) if a or b else (other,):
                pltpu.make_async_remote_copy(
                    src_ref=outgoing.at[0],
                    dst_ref=arrived.at[a, b, core],
                    send_sem=in_send.at[0, 0],
                    recv_sem=in_recv.at[core, a * count_lo + b],
                    device_id={"cuts": other},
                    device_id_type=MESH,
                ).wait_recv()
        piece = jnp.concatenate(
            [arrived[a, b].reshape(wide, span_lo) for b in range(count_lo)], axis=1
        )
        high, low = halves(piece)
        parts = []
        for s in range(2 * turns):
            part = dot(high, second_ref[0, s]) + dot(low, second_ref[0, s]) + dot(high, second_ref[1, s])
            for z in range(CLOSED):
                parts.append(part[z * span_hi : (z + 1) * span_hi] * rears[s][z : z + 1])
        high, low = halves(jnp.concatenate(parts, axis=0))

        def side_sum(side):
            left, rest = first_ref[0, a, side], first_ref[1, a, side]
            return dot(left, high) + dot(left, low) + dot(rest, high)

        return side_sum

    for a in range(half - 1):
        side_sum = advance(a)
        for side in range(2):
            if a == 0:
                sums[side] = side_sum(side)
            else:
                sums[side] += side_sum(side)
    side_sum = advance(half - 1)
    outs = []
    for side in (1, 0):
        total = sums[side] + side_sum(side) if half > 1 else side_sum(side)
        for e in range(count_lo):
            result[side, e] = total[:, e * span_lo : (e + 1) * span_lo]
        if side:

            @pl.when(upper == 0)
            def _():
                pl.semaphore_wait(ready, blocks)

        for a, b in near:
            ra, rb = inner ^ a, lo ^ b
            spot = ra * count_lo + rb
            for core in range(CLOSED):
                copy = pltpu.make_async_remote_copy(
                    src_ref=result.at[
                        side, b, pl.ds(pl.multiple_of(ra * span_hi + core * per, per), per)
                    ],
                    dst_ref=landed.at[side, spot, cut],
                    send_sem=out_send.at[side, a * count_lo + b, core],
                    recv_sem=out_recv.at[side, spot, cut],
                    device_id={"hi": flipped(upper, side) * half + a, "lo": b, "cuts": core},
                    device_id_type=MESH,
                )
                outs.append((side, a, b, core, copy))
                if side:
                    copy.start()
                else:
                    pl.when((spot > 0) | (cut != core))(copy.start)
    for a, b in near:
        k = a * count_lo + b
        for core in range(CLOSED) if a or b else (other, cut):
            for side in range(2):
                if side or a or b or core is other:
                    pltpu.make_async_remote_copy(
                        src_ref=result.at[0, 0, pl.ds(0, per)],
                        dst_ref=landed.at[side, k, core],
                        send_sem=out_send.at[0, 0, 0],
                        recv_sem=out_recv.at[side, k, core],
                        device_id={"cuts": other},
                        device_id_type=MESH,
                    ).wait_recv()
            if a or b or core is other:
                mine = landed[0, k, core]
            else:
                mine = result[0, lo, pl.ds(pl.multiple_of(cut * per, per), per), :]
            out_ref[pl.ds(block(a, b, core), per, stride=blocks), :] = mine + landed[1, k, core]
    for copy in sends:
        copy.wait_send()
    for side, a, b, core, copy in outs:
        if side:
            copy.wait_send()
        else:
            pl.when(((inner ^ a) > 0) | ((lo ^ b) > 0) | (cut != core))(copy.wait_send)


def local(state_block, gate_table, closing_table, slice_edges, bit_orders):
    count_hi = lax.axis_size("hi")
    count_lo = lax.axis_size("lo")
    span_hi = GATE // count_hi
    span_lo = GATE // count_lo
    blocks = count_hi * count_lo
    half = count_hi // 2
    middle = state_block.shape[2] // (GATE * GATE * CLOSED)
    fits = middle == 1 and span_lo == 128 and span_hi % 16 == 0 and count_hi % 2 == 0
    if not fits or lax.axis_size("cuts") != CLOSED:
        return local_plain(state_block, gate_table, closing_table, slice_edges, bit_orders)
    slices = slice_edges.shape[0] * CLOSED
    rows = GATE // 2
    per = span_hi // 2
    hbm = pl.BlockSpec(memory_space=pltpu.HBM)
    dma = pltpu.SemaphoreType.DMA
    out = pl.pallas_call(
        functools.partial(kernel, count_hi, count_lo),
        out_shape=jax.ShapeDtypeStruct((per * blocks, span_lo), FULL),
        in_specs=[hbm] * 5,
        out_specs=pl.BlockSpec(memory_space=pltpu.VMEM),
        scratch_shapes=[
            pltpu.VMEM((span_hi * blocks * CLOSED, span_lo), FULL),
            pltpu.VMEM(gate_table.shape, FULL),
            pltpu.VMEM(closing_table.shape, FULL),
            pltpu.VMEM(slice_edges.shape, jnp.int32),
            pltpu.SMEM(bit_orders.shape, jnp.int32),
            pltpu.VMEM((blocks, span_hi, span_lo), FULL),
            pltpu.VMEM((half, count_lo, CLOSED, span_hi, span_lo), FULL),
            pltpu.VMEM(slice_edges.shape, jnp.int32),
            pltpu.VMEM((2, half, 2, rows, slices * CLOSED * span_hi), HALF),
            pltpu.VMEM((2, slices, GATE, GATE), HALF),
            pltpu.VMEM((2, rows, GATE), FULL),
            pltpu.VMEM((2, count_lo, rows, span_lo), FULL),
            pltpu.VMEM((2, half * count_lo, CLOSED, per, span_lo), FULL),
            dma((5,)),
            dma((2,)),
            pltpu.SemaphoreType.REGULAR,
            dma((CLOSED, half * count_lo)),
            dma((CLOSED, half * count_lo)),
            dma((2, half * count_lo, CLOSED)),
            dma((2, half * count_lo, CLOSED)),
        ],
        compiler_params=pltpu.CompilerParams(
            collective_id=0, has_side_effects=True, vmem_limit_bytes=32 * 1024 * 1024
        ),
    )(
        *(
            pltpu.with_memory_space_constraint(item, pltpu.HBM)
            for item in (
                state_block.reshape(-1, span_lo),
                gate_table,
                closing_table,
                slice_edges,
                bit_orders,
            )
        )
    )
    return out.reshape(1, 1, -1)


def solution(mesh):
    in_specs = (P(("group", "hi"), "lo", None), P(), P(), P(("group", "cuts"), None), P())
    out_specs = P(("group", "hi"), "lo", "cuts")
    return jax.shard_map(local, mesh=mesh, in_specs=in_specs, out_specs=out_specs, check_vma=False)
```

time: 19.8 us -> 17.9 us (0.904)
  the two profiles are of different devices: /device:TPU:1 before, /device:TPU:0 now
where the time goes in v1:
time: 17.9 us; the launch traced here: 17.8 us
  Pallas kernels  17.1 us (96%)
  local copies, waits for them, and re-layouts  0.66 us (4%)
    pallas_call x1, Pallas kernels, local(): pl.pallas_call(functools.partial(kernel, count_hi, count_lo), out_shape=j...  17.1 us
    unnamed x1, local copies, waits for them, and re-layouts  0.66 us

profile of v1, /device:TPU:0, one launch (start us, length us, event | category | flops | bytes accessed | tf_op | source)
XLA Modules:
  0.0 17.8 jit_solution(842536398632666333)
XLA Ops:
  0.0 17.1 %shard_map.55 = f32[256,128]{1,0:T(8,128)S(1)} custom-call(f32[1024,128]{1,0:T(8,128)} %bitcast.3, f32[4,256,256]{2,1,0:T(8,128)} %gate_hbm.1, f32[4,2,2,256]{3,2,1,0:T(2,128)} %closing_hbm.1, s32[2,3]{1,0:T(2,128)} %edges_hbm.1, s32[2,8]{1,0:T(2,128)} %orders_hbm.1), custom_call_target="tpu_custom_call" | custom-call | tf_op jit(solution)/shard_map/pallas_call | solution.py:400
  17.1 0.7 %copy.7 = f32[1,1,32768]{2,1,0:T(1,128)} copy(f32[1,1,32768]{2,1,0:T(1,128)S(1)} %bitcast.2) | data formatting | bytes 262144

commit v2 on v1

--- a/solution.py
+++ b/solution.py
@@ -8,6 +8,8 @@
 from jax.sharding import PartitionSpec as P
 
 BITS = 8
+STEPS = ((1, 0, 3, 2), (3, 2, 0, 1))
+ORDERS = ("SWF", "SWF")
 GATE = 256
 CLOSED = 2
 
@@ -157,6 +159,41 @@
     turns = edges_ref.shape[0]
     edges = gate_ref.shape[0]
     near = [(a, b) for a in range(half) for b in range(count_lo)]
+    cores = [(a, b, core) for a, b in near for core in range(CLOSED)]
+
+    def keeper(a, b, core):
+        if core == CLOSED - 1 and a == half - 1:
+            return 0
+        if core == CLOSED - 1 and b == 1:
+            return 1
+        return None
+
+    def holder(a, core, half_index):
+        return a
+
+    def here(a, b, core):
+        return (inner == holder(a, core, upper)) & (lo == b) & (cut == core)
+
+    def any_of(half_index):
+        return functools.reduce(
+            lambda p, q: p | q,
+            [here(*spot) for spot in cores if keeper(*spot) == half_index],
+            hi < 0,
+        )
+
+    kept = [any_of(0), any_of(1)]
+    wide_role = (kept[0] & (upper == 0)) | (kept[1] & (upper == 1))
+    idle = (kept[0] & (upper == 1)) | (kept[1] & (upper == 0))
+    slots = []
+    for spot in cores:
+        done = sum(keeper(*item) is None for item in cores[: len(slots)])
+        slots.append((len(slots), len(cores) + done))
+    mine = [0, 0]
+    for spot, pair in zip(cores, slots):
+        for side in range(2):
+            index = pair[side if keeper(*spot) is None else 0]
+            mine[side] += here(*spot).astype(jnp.int32) * index
+    taken = len(cores) + sum(keeper(*spot) is None for spot in cores)
     pairs = (
         (x_hbm, x_ref),
         (edges_hbm, edges_ref),
@@ -172,9 +209,6 @@
         th = flipped(upper, side) * half + flipped(inner, a)
         return {"hi": th, "lo": flipped(lo, b), "cuts": core}
 
-    def block(a, b, core):
-        return (flipped(inner, a) * CLOSED + core) * count_lo + flipped(lo, b)
-
     def greet(semaphore, side):
         for a, b in near:
             for core in range(CLOSED):
@@ -187,7 +221,7 @@
     pl.semaphore_signal(barrier, inc=1, device_id={"cuts": other}, device_id_type=MESH)
     greet(barrier, 0)
 
-    @pl.when(upper == 0)
+    @pl.when((upper == 0) | kept[1])
     def _():
         greet(barrier, 1)
 
@@ -197,33 +231,36 @@
         for e in range(count_lo):
             start = b * CLOSED * count_lo + cut * count_lo + e
             outgoing[b * count_lo + e] = x_ref[pl.ds(start, span_hi, stride=stride), :]
-    arrived[0, 0, cut] = outgoing[block(0, 0, cut)]
-    pl.semaphore_wait(barrier, blocks - 1 + upper * blocks)
-
-    sends = []
-    for core in range(CLOSED):
-        for a, b in sorted(near[1:], key=lambda spot: (spot[0] > 0, spot[1] == 0)):
-            k = a * count_lo + b
-            copy = pltpu.make_async_remote_copy(
-                src_ref=outgoing.at[block(a, b, core)],
-                dst_ref=arrived.at[a, b, cut],
-                send_sem=in_send.at[core, k],
-                recv_sem=in_recv.at[cut, k],
-                device_id=device(0, a, b, core),
-                device_id_type=MESH,
-            )
-            copy.start()
-            sends.append(copy)
-    copy = pltpu.make_async_remote_copy(
-        src_ref=outgoing.at[block(0, 0, other)],
-        dst_ref=arrived.at[0, 0, cut],
-        send_sem=in_send.at[0, 0],
-        recv_sem=in_recv.at[cut, 0],
-        device_id={"cuts": other},
-        device_id_type=MESH,
+    guests = sum(keeper(*spot) == 1 for spot in cores)
+    pl.semaphore_wait(barrier, blocks - 1 + jnp.where(upper == 1, blocks, guests))
+
+    for half_index, order in enumerate(ORDERS):
+        for group in order:
+            for a, b, core in cores:
+                keep = keeper(a, b, core)
+                kind = "S" if keep is None else "W" if keep == half_index else "F"
+                if kind != group:
+                    continue
+                goal_half = half_index if keep is None else keep
+                goal = holder(a, core, goal_half)
+                k = (inner ^ goal) + (half if kind == "F" else 0)
+                copy = pltpu.make_async_remote_copy(
+                    src_ref=outgoing.at[(a * CLOSED + core) * count_lo + b],
+                    dst_ref=arrived.at[k, lo ^ b, cut],
+                    send_sem=in_send,
+                    recv_sem=in_recv.at[k],
+                    device_id={"hi": goal + goal_half * half, "lo": b, "cuts": core},
+                    device_id_type=MESH,
+                )
+                away = upper == half_index
+                if kind != "F":
+                    away = away & ~here(a, b, core)
+                pl.when(away)(copy.start)
+    own = holder(inner, cut, upper)
+    own_copy = pltpu.make_async_copy(
+        outgoing.at[(own * CLOSED + cut) * count_lo + lo], arrived.at[0, 0, cut], in_recv.at[0]
     )
-    copy.start()
-    sends.append(copy)
+    pl.when(~idle)(own_copy.start)
 
     gets[1].wait()
     edge_copy = pltpu.make_async_remote_copy(
@@ -249,8 +286,7 @@
 
     column = down % span_hi * count_hi + high_bits(down // rows, down % rows // span_hi)
     columns = (column == along).astype(FULL).astype(HALF)
-    row = down % span_hi * count_hi + high_bits(0, down % rows // span_hi)
-    rows_one = (source_row(row[:rows], orders_ref, 0) == along[:rows]).astype(FULL).astype(HALF)
+    rows_one = (source_row(column, orders_ref, 0) == along).astype(FULL).astype(HALF)
     row = (down // span_lo ^ lo) * span_lo + down % span_lo
     rows_two = (source_row(row, orders_ref, 1) == along).astype(FULL).astype(HALF)
 
@@ -258,127 +294,160 @@
     gets[4].wait()
     edge_copy.wait()
     wide = CLOSED * span_hi
-    rears = []
-    for s in range(2 * turns):
+
+    def pick(s, place, values):
         chosen = edges_ref if s < turns else edges_far
         turn = s % turns
-
-        def pick(place, values):
-            total = None
-            for c in range(edges):
-                weight = (chosen[turn : turn + 1, place : place + 1] == c).astype(FULL)
-                term = weight * values(c)
-                total = term if total is None else total + term
-            return total
-
-        rears.append(pick(2, lambda c: closing_ref[c, 1]))
-        fronts = pick(2, lambda c: closing_ref[c, 0])
-        gate = pick(0, lambda c: gate_ref[c])
+        total = None
+        for c in range(edges):
+            weight = (chosen[turn : turn + 1, place : place + 1] == c).astype(FULL)
+            term = weight * values(c)
+            total = term if total is None else total + term
+        return total
+
+    def build_first(s, far):
+        fronts = pick(s, 2, lambda c: closing_ref[c, 0])
+        gate = pick(s, 0, lambda c: gate_ref[c])
         split = [halves(gate * fronts[z : z + 1]) for z in range(CLOSED)]
+        chosen_rows = rows_one[far * rows : (far + 1) * rows]
         for part in range(2):
-            moved = [dot(rows_one, split[z][part]).astype(HALF) for z in range(CLOSED)]
+            moved = [dot(chosen_rows, split[z][part]).astype(HALF) for z in range(CLOSED)]
             moved = dot(columns, jnp.concatenate(moved, axis=0), ((1,), (1,))).astype(HALF)
             for side in range(2):
                 for a in range(half):
                     for z in range(CLOSED):
                         start = z * rows + a * span_hi
                         first_ref[
-                            part, a, side, :, s * wide + z * span_hi : s * wide + (z + 1) * span_hi
+                            far * half + a,
+                            side,
+                            part * rows : (part + 1) * rows,
+                            s * wide + z * span_hi : s * wide + (z + 1) * span_hi,
                         ] = moved[side * rows : (side + 1) * rows, start : start + span_hi]
-        for part, piece in enumerate(halves(pick(1, lambda c: gate_ref[c]))):
+
+    rears = []
+    for s in range(2 * turns):
+        rears.append(pick(s, 2, lambda c: closing_ref[c, 1]))
+        build_first(s, 0)
+        for part, piece in enumerate(halves(pick(s, 1, lambda c: gate_ref[c]))):
             second_ref[part, s] = dot(rows_two, piece).astype(HALF)
 
+    @pl.when(wide_role)
+    def _():
+        for s in range(2 * turns):
+            build_first(s, 1)
+
     def advance(a):
-        for b in range(count_lo):
-            for core in range(CLOSED) if a or b else (other,):
-                pltpu.make_async_remote_copy(
-                    src_ref=outgoing.at[0],
-                    dst_ref=arrived.at[a, b, core],
-                    send_sem=in_send.at[0, 0],
-                    recv_sem=in_recv.at[core, a * count_lo + b],
-                    device_id={"cuts": other},
-                    device_id_type=MESH,
-                ).wait_recv()
+        pltpu.make_async_copy(arrived.at[a], arrived.at[a], in_recv.at[a]).wait()
         piece = jnp.concatenate(
             [arrived[a, b].reshape(wide, span_lo) for b in range(count_lo)], axis=1
         )
         high, low = halves(piece)
+        pair = jnp.concatenate([high, low], axis=0)
         parts = []
         for s in range(2 * turns):
-            part = dot(high, second_ref[0, s]) + dot(low, second_ref[0, s]) + dot(high, second_ref[1, s])
+            both = dot(pair, second_ref[0, s])
+            part = both[:wide] + both[wide:] + dot(high, second_ref[1, s])
             for z in range(CLOSED):
                 parts.append(part[z * span_hi : (z + 1) * span_hi] * rears[s][z : z + 1])
         high, low = halves(jnp.concatenate(parts, axis=0))
 
         def side_sum(side):
-            left, rest = first_ref[0, a, side], first_ref[1, a, side]
-            return dot(left, high) + dot(left, low) + dot(rest, high)
+            both = dot(first_ref[a, side], high)
+            return both[:rows] + both[rows:] + dot(first_ref[a, side, :rows, :], low)
 
         return side_sum
 
-    for a in range(half - 1):
+    def gather(a, start=False):
         side_sum = advance(a)
         for side in range(2):
-            if a == 0:
+            if start:
                 sums[side] = side_sum(side)
             else:
                 sums[side] += side_sum(side)
-    side_sum = advance(half - 1)
+
     outs = []
-    for side in (1, 0):
-        total = sums[side] + side_sum(side) if half > 1 else side_sum(side)
-        for e in range(count_lo):
-            result[side, e] = total[:, e * span_lo : (e + 1) * span_lo]
-        if side:
-
-            @pl.when(upper == 0)
-            def _():
-                pl.semaphore_wait(ready, blocks)
-
-        for a, b in near:
-            ra, rb = inner ^ a, lo ^ b
-            spot = ra * count_lo + rb
-            for core in range(CLOSED):
-                copy = pltpu.make_async_remote_copy(
-                    src_ref=result.at[
-                        side, b, pl.ds(pl.multiple_of(ra * span_hi + core * per, per), per)
-                    ],
-                    dst_ref=landed.at[side, spot, cut],
-                    send_sem=out_send.at[side, a * count_lo + b, core],
-                    recv_sem=out_recv.at[side, spot, cut],
-                    device_id={"hi": flipped(upper, side) * half + a, "lo": b, "cuts": core},
-                    device_id_type=MESH,
-                )
-                outs.append((side, a, b, core, copy))
-                if side:
-                    copy.start()
-                else:
-                    pl.when((spot > 0) | (cut != core))(copy.start)
-    for a, b in near:
-        k = a * count_lo + b
-        for core in range(CLOSED) if a or b else (other, cut):
-            for side in range(2):
-                if side or a or b or core is other:
-                    pltpu.make_async_remote_copy(
-                        src_ref=result.at[0, 0, pl.ds(0, per)],
-                        dst_ref=landed.at[side, k, core],
-                        send_sem=out_send.at[0, 0, 0],
-                        recv_sem=out_recv.at[side, k, core],
-                        device_id={"cuts": other},
-                        device_id_type=MESH,
-                    ).wait_recv()
-            if a or b or core is other:
-                mine = landed[0, k, core]
-            else:
-                mine = result[0, lo, pl.ds(pl.multiple_of(cut * per, per), per), :]
-            out_ref[pl.ds(block(a, b, core), per, stride=blocks), :] = mine + landed[1, k, core]
-    for copy in sends:
-        copy.wait_send()
-    for side, a, b, core, copy in outs:
-        if side:
-            copy.wait_send()
+    for goal in range(2):
+        side = goal ^ upper
+        for a, b, core in cores if goal == 0 else sorted(cores, key=lambda spot: -spot[0]):
+            source = result.at[
+                goal, b, pl.ds(pl.multiple_of((inner ^ a) * span_hi + core * per, per), per)
+            ]
+            target = landed.at[jnp.where(side == 0, mine[0], mine[1])]
+            copy = pltpu.make_async_remote_copy(
+                src_ref=source,
+                dst_ref=target,
+                send_sem=out_send,
+                recv_sem=out_recv,
+                device_id={"hi": goal * half + a, "lo": b, "cuts": core},
+                device_id_type=MESH,
+            )
+            at_home = (upper == goal) & (inner == a) & (lo == b) & (cut == core)
+            outs.append((goal, ~at_home, copy))
+
+    def finish(a):
+        side_sum = advance(a)
+        for goal in range(2):
+            side = goal ^ upper
+            total = sums[side] + side_sum(side)
+            for e in range(count_lo):
+                result[goal, e] = total[:, e * span_lo : (e + 1) * span_lo]
+            if goal:
+
+                @pl.when(upper == 0)
+                def _():
+                    pl.semaphore_wait(ready, blocks)
+
+            for order, away, copy in outs:
+                if order == goal:
+                    pl.when(away)(copy.start)
+        pltpu.make_async_copy(
+            result.at[upper, lo, pl.ds(pl.multiple_of((cut * per), per), per)],
+            landed.at[mine[0]],
+            out_recv,
+        ).start()
+
+    @pl.when(~wide_role & ~idle)
+    def _():
+        for a in range(half - 1):
+            gather(a, a == 0)
+        finish(half - 1)
+
+    @pl.when(kept[0] & (upper == 0))
+    def _():
+        for a in STEPS[0][:-1]:
+            gather(a, a == STEPS[0][0])
+        finish(STEPS[0][-1])
+
+    @pl.when(kept[1] & (upper == 1))
+    def _():
+        for a in STEPS[1][:-1]:
+            gather(a, a == STEPS[1][0])
+        finish(STEPS[1][-1])
+
+    @pl.when(idle & (upper == 0))
+    def _():
+        pl.semaphore_wait(ready, blocks)
+
+    arrivals = landed.at[pl.ds(0, taken)]
+
+    pltpu.make_async_copy(arrivals, arrivals, out_recv).wait()
+    for (a, b, core), (first, second) in zip(cores, slots):
+        place = pl.ds((a * CLOSED + core) * count_lo + b, per, stride=blocks)
+        if keeper(a, b, core) is not None:
+            out_ref[place, :] = landed[first]
         else:
-            pl.when(((inner ^ a) > 0) | ((lo ^ b) > 0) | (cut != core))(copy.wait_send)
+            out_ref[place, :] = landed[first] + landed[second]
+    gone = outgoing.at[pl.ds(0, blocks - 1)]
+    pltpu.make_async_copy(gone, gone, in_send).wait()
+
+    @pl.when(idle)
+    def _():
+        pltpu.make_async_copy(outgoing.at[0], outgoing.at[0], in_send).wait()
+
+    @pl.when(~idle)
+    def _():
+        gone = landed.at[pl.ds(0, 2 * blocks - 1)]
+        pltpu.make_async_copy(gone, gone, out_send).wait()
 
 
 def local(state_block, gate_table, closing_table, slice_edges, bit_orders):
@@ -409,20 +478,20 @@
             pltpu.VMEM(slice_edges.shape, jnp.int32),
             pltpu.SMEM(bit_orders.shape, jnp.int32),
             pltpu.VMEM((blocks, span_hi, span_lo), FULL),
-            pltpu.VMEM((half, count_lo, CLOSED, span_hi, span_lo), FULL),
+            pltpu.VMEM((count_hi, count_lo, CLOSED, span_hi, span_lo), FULL),
             pltpu.VMEM(slice_edges.shape, jnp.int32),
-            pltpu.VMEM((2, half, 2, rows, slices * CLOSED * span_hi), HALF),
+            pltpu.VMEM((count_hi, 2, 2 * rows, slices * CLOSED * span_hi), HALF),
             pltpu.VMEM((2, slices, GATE, GATE), HALF),
             pltpu.VMEM((2, rows, GATE), FULL),
             pltpu.VMEM((2, count_lo, rows, span_lo), FULL),
-            pltpu.VMEM((2, half * count_lo, CLOSED, per, span_lo), FULL),
+            pltpu.VMEM((2 * blocks, per, span_lo), FULL),
             dma((5,)),
             dma((2,)),
             pltpu.SemaphoreType.REGULAR,
-            dma((CLOSED, half * count_lo)),
-            dma((CLOSED, half * count_lo)),
-            dma((2, half * count_lo, CLOSED)),
-            dma((2, half * count_lo, CLOSED)),
+            dma(()),
+            dma((count_hi,)),
+            dma(()),
+            dma(()),
         ],
         compiler_params=pltpu.CompilerParams(
             collective_id=0, has_side_effects=True, vmem_limit_bytes=32 * 1024 * 1024

time: 17.9 us -> 16.7 us (0.933)
  Pallas kernels: 17.1 us -> 15.8 us
    pallas_call x1, Pallas kernels: 17.1 us -> 15.8 us  [local(): pl.pallas_call(functools.partial(kernel, count_hi, count_lo), out_shape=j...]
where the time goes in v2:
time: 16.7 us; the launch traced here: 16.5 us
  Pallas kernels  15.8 us (95%)
  local copies, waits for them, and re-layouts  0.66 us (4%)
    pallas_call x1, Pallas kernels, local(): pl.pallas_call(functools.partial(kernel, count_hi, count_lo), out_shape=j...  15.8 us
    unnamed x1, local copies, waits for them, and re-layouts  0.66 us

profile of v2, /device:TPU:0, one launch (start us, length us, event | category | flops | bytes accessed | tf_op | source)
XLA Modules:
  0.0 16.5 jit_solution(5344320713102081817)
XLA Ops:
  0.0 15.8 %shard_map.55 = f32[256,128]{1,0:T(8,128)S(1)} custom-call(f32[1024,128]{1,0:T(8,128)} %bitcast.3, f32[4,256,256]{2,1,0:T(8,128)} %gate_hbm.1, f32[4,2,2,256]{3,2,1,0:T(2,128)} %closing_hbm.1, s32[2,3]{1,0:T(2,128)} %edges_hbm.1, s32[2,8]{1,0:T(2,128)} %orders_hbm.1), custom_call_target="tpu_custom_call" | custom-call | tf_op jit(solution)/shard_map/pallas_call | solution.py:469
  15.9 0.7 %copy.7 = f32[1,1,32768]{2,1,0:T(1,128)} copy(f32[1,1,32768]{2,1,0:T(1,128)S(1)} %bitcast.2) | data formatting | bytes 262144

commit v3 on v2

--- a/solution.py
+++ b/solution.py
@@ -8,8 +8,8 @@
 from jax.sharding import PartitionSpec as P
 
 BITS = 8
-STEPS = ((1, 0, 3, 2), (3, 2, 0, 1))
-ORDERS = ("SWF", "SWF")
+STEPS = ((3, 0, 1, 2), (3, 0, 2, 1))
+ORDERS = ("SWF", "SFW")
 GATE = 256
 CLOSED = 2
 
@@ -368,7 +368,7 @@
     outs = []
     for goal in range(2):
         side = goal ^ upper
-        for a, b, core in cores if goal == 0 else sorted(cores, key=lambda spot: -spot[0]):
+        for a, b, core in cores if goal == 0 else sorted(cores, key=lambda spot: (-spot[0], -spot[1])):
             source = result.at[
                 goal, b, pl.ds(pl.multiple_of((inner ^ a) * span_hi + core * per, per), per)
             ]

time: 16.7 us -> 16.3 us (0.976)
  Pallas kernels: 15.8 us -> 15.5 us
    pallas_call x1, Pallas kernels: 15.8 us -> 15.5 us  [local(): pl.pallas_call(functools.partial(kernel, count_hi, count_lo), out_shape=j...]
where the time goes in v3:
time: 16.3 us; the launch traced here: 16.2 us
  Pallas kernels  15.5 us (95%)
  local copies, waits for them, and re-layouts  0.66 us (4%)
    pallas_call x1, Pallas kernels, local(): pl.pallas_call(functools.partial(kernel, count_hi, count_lo), out_shape=j...  15.5 us
    unnamed x1, local copies, waits for them, and re-layouts  0.66 us

profile of v3, /device:TPU:0, one launch (start us, length us, event | category | flops | bytes accessed | tf_op | source)
XLA Modules:
  0.0 16.2 jit_solution(1288418560604018718)
XLA Ops:
  0.0 15.5 %shard_map.55 = f32[256,128]{1,0:T(8,128)S(1)} custom-call(f32[1024,128]{1,0:T(8,128)} %bitcast.3, f32[4,256,256]{2,1,0:T(8,128)} %gate_hbm.1, f32[4,2,2,256]{3,2,1,0:T(2,128)} %closing_hbm.1, s32[2,3]{1,0:T(2,128)} %edges_hbm.1, s32[2,8]{1,0:T(2,128)} %orders_hbm.1), custom_call_target="tpu_custom_call" | custom-call | tf_op jit(solution)/shard_map/pallas_call | solution.py:469
  15.5 0.7 %copy.7 = f32[1,1,32768]{2,1,0:T(1,128)} copy(f32[1,1,32768]{2,1,0:T(1,128)S(1)} %bitcast.2) | data formatting | bytes 262144

commit v4 on v3

--- a/solution.py
+++ b/solution.py
@@ -458,7 +458,7 @@
     blocks = count_hi * count_lo
     half = count_hi // 2
     middle = state_block.shape[2] // (GATE * GATE * CLOSED)
-    fits = middle == 1 and span_lo == 128 and span_hi % 16 == 0 and count_hi % 2 == 0
+    fits = middle == 1 and span_lo == 128 and span_hi % 16 == 0 and count_hi == len(STEPS[0])
     if not fits or lax.axis_size("cuts") != CLOSED:
         return local_plain(state_block, gate_table, closing_table, slice_edges, bit_orders)
     slices = slice_edges.shape[0] * CLOSED

time: 16.3 us -> 16.3 us (level)
  no operation moved by 1% of the time
where the time goes in v4:
time: 16.3 us; the launch traced here: 16.2 us
  Pallas kernels  15.5 us (95%)
  local copies, waits for them, and re-layouts  0.66 us (4%)
    pallas_call x1, Pallas kernels, local(): pl.pallas_call(functools.partial(kernel, count_hi, count_lo), out_shape=j...  15.5 us
    unnamed x1, local copies, waits for them, and re-layouts  0.66 us

profile of v4, /device:TPU:0, one launch (start us, length us, event | category | flops | bytes accessed | tf_op | source)
XLA Modules:
  0.0 16.2 jit_solution(1288418560604018718)
XLA Ops:
  0.0 15.5 %shard_map.55 = f32[256,128]{1,0:T(8,128)S(1)} custom-call(f32[1024,128]{1,0:T(8,128)} %bitcast.3, f32[4,256,256]{2,1,0:T(8,128)} %gate_hbm.1, f32[4,2,2,256]{3,2,1,0:T(2,128)} %closing_hbm.1, s32[2,3]{1,0:T(2,128)} %edges_hbm.1, s32[2,8]{1,0:T(2,128)} %orders_hbm.1), custom_call_target="tpu_custom_call" | custom-call | tf_op jit(solution)/shard_map/pallas_call | solution.py:469
  15.5 0.7 %copy.7 = f32[1,1,32768]{2,1,0:T(1,128)} copy(f32[1,1,32768]{2,1,0:T(1,128)S(1)} %bitcast.2) | data formatting | bytes 262144

commit v5 on v4

--- a/solution.py
+++ b/solution.py
@@ -9,7 +9,7 @@
 
 BITS = 8
 STEPS = ((3, 0, 1, 2), (3, 0, 2, 1))
-ORDERS = ("SWF", "SFW")
+ORDERS = ("SFW", "SFW")
 GATE = 256
 CLOSED = 2
 

time: 16.3 us -> 16.3 us (level)
  no operation moved by 1% of the time
where the time goes in v5:
time: 16.3 us; the launch traced here: 16.2 us
  Pallas kernels  15.5 us (95%)
  local copies, waits for them, and re-layouts  0.66 us (4%)
    pallas_call x1, Pallas kernels, local(): pl.pallas_call(functools.partial(kernel, count_hi, count_lo), out_shape=j...  15.5 us
    unnamed x1, local copies, waits for them, and re-layouts  0.66 us

profile of v5, /device:TPU:0, one launch (start us, length us, event | category | flops | bytes accessed | tf_op | source)
XLA Modules:
  0.0 16.2 jit_solution(3844995394368889170)
XLA Ops:
  0.0 15.5 %shard_map.55 = f32[256,128]{1,0:T(8,128)S(1)} custom-call(f32[1024,128]{1,0:T(8,128)} %bitcast.3, f32[4,256,256]{2,1,0:T(8,128)} %gate_hbm.1, f32[4,2,2,256]{3,2,1,0:T(2,128)} %closing_hbm.1, s32[2,3]{1,0:T(2,128)} %edges_hbm.1, s32[2,8]{1,0:T(2,128)} %orders_hbm.1), custom_call_target="tpu_custom_call" | custom-call | tf_op jit(solution)/shard_map/pallas_call | solution.py:469
  15.5 0.7 %copy.7 = f32[1,1,32768]{2,1,0:T(1,128)} copy(f32[1,1,32768]{2,1,0:T(1,128)S(1)} %bitcast.2) | data formatting | bytes 262144
